TPU v7x, 32 devices: a whole 2x2x4 slice. The times are simulated.
32 devices in a mesh: row: 4 (over y, x), col: 8 (over z, core).
Axes of the slice: x: 2, y: 2, z: 4, core: 2. Of those that a mesh axis runs over, the one named last changes fastest.
Arguments:
- view_a: bfloat16 [3072, 8192], P(('row', 'col')), may hold values from -1000 to 1000
- view_b: bfloat16 [3072, 8192], P(('row', 'col')), may hold values from -1000 to 1000
Outputs:
- correlation: float32 [8192, 8192], P('row', 'col')
- loss: float32 [], replicated
All inputs are finite; a program needn't handle non-finite values.
Results may differ from a plain program's by a relative error of at most 0.0013.
Values may be sent and summed in bfloat16 or wider, within the bound.
A program may use at most 192 MiB of HBM per device.

v0:
```python
import functools

import jax
import jax.numpy as jnp
from jax import lax
from jax.experimental import pallas as pl
from jax.experimental.pallas import tpu as pltpu
from jax.sharding import PartitionSpec as P

MESH = pl.DeviceIdType.MESH
F32 = jnp.float32
BF16 = jnp.bfloat16


def body(
    n_row, n_col, width,
    a_in, b_in, out, loss_out,
    a_all, b_all, nb, stat_a, stat_b, coef_a, coef_b, loss_row, loss_col,
    s_a, r_a, s_b, r_b, s_sa, r_sa, s_sb, r_sb, s_line, r_line, s_fwd, r_fwd,
    s_lr, r_lr, s_lc, r_lc, own_sem,
):
    t = a_in.shape[0]
    rb = a_in.shape[1] // n_row
    cb = b_in.shape[1] // n_col
    count = t * n_row * n_col
    n_z = n_col // 2
    r = lax.axis_index("row")
    c = lax.axis_index("col")
    z = c // 2
    k = c % 2
    mine = pl.ds(pl.multiple_of(r * t, t), t)

    def row_mate(i):
        return (r + i) % n_row

    def col_mate(j):
        return (c + j) % n_col

    def remote(src, dst, ss, rs, dev):
        return pltpu.make_async_remote_copy(
            src_ref=src, dst_ref=dst, send_sem=ss, recv_sem=rs, device_id=dev, device_id_type=MESH
        )

    own_a = pltpu.make_async_copy(
        a_in.at[:, pl.ds(pl.multiple_of(r * rb, rb), rb)], a_all.at[c, mine], own_sem.at[0]
    )
    own_b = pltpu.make_async_copy(
        b_in.at[:, pl.ds(pl.multiple_of(c * cb, cb), cb)], b_all.at[c, mine], own_sem.at[1]
    )
    own_a.start()
    own_b.start()

    barrier = pltpu.get_barrier_semaphore()
    for i in range(1, n_row):
        pl.semaphore_signal(barrier, inc=1, device_id=(row_mate(i), c), device_id_type=MESH)
    for j in range(1, n_col):
        pl.semaphore_signal(barrier, inc=1, device_id=(r, col_mate(j)), device_id_type=MESH)
    pl.semaphore_wait(barrier, n_row + n_col - 2)

    def send_a(i):
        dst = row_mate(i)
        cols = pl.ds(pl.multiple_of(dst * rb, rb), rb)
        return remote(a_in.at[:, cols], a_all.at[c, mine], s_a.at[i], r_a.at[i], (dst, c))

    def got_a(i):
        src = row_mate(n_row - i)
        rows = pl.ds(pl.multiple_of(src * t, t), t)
        return remote(a_all.at[c, rows], a_all.at[c, rows], s_a.at[i], r_a.at[i], (src, c))

    def send_b(j):
        dst = col_mate(j)
        cols = pl.ds(pl.multiple_of(dst * cb, cb), cb)
        return remote(b_in.at[:, cols], b_all.at[c, mine], s_b.at[j], r_b.at[j], (r, dst))

    def got_b(j):
        src = col_mate(n_col - j)
        return remote(b_all.at[src, mine], b_all.at[src, mine], s_b.at[j], r_b.at[j], (r, src))

    for i in range(1, n_row):
        send_a(i).start()

    def line(way, chunk, p, dev_c):
        rows = pl.ds(pl.multiple_of(p * t, t), t)
        ref = a_all.at[chunk, rows]
        return remote(ref, ref, s_line.at[way, chunk, p], r_line.at[chunk, p], (r, dev_c))

    partner = z * 2 + (1 - k)

    def up(chunk, p):
        return line(0, chunk, p, lax.min(c + 2, n_col - 2 + k))

    def down(chunk, p):
        return line(1, chunk, p, lax.max(c - 2, k))

    def across(chunk, p):
        return line(2, chunk, p, partner)

    can_up = z < n_z - 1
    can_down = z > 0

    def slice_at(o):
        return (r + n_row - o) % n_row

    def send_line(o):
        p = slice_at(o)

        @pl.when(can_up)
        def _():
            up(c, p).start()

        @pl.when(can_down)
        def _():
            down(c, p).start()

        across(c, p).start()

    own_a.wait()
    send_line(0)

    for dist in range(n_z - 1, 0, -1):
        for side in range(2):
            zz = z - dist if side == 0 else z + dist

            @pl.when(jnp.logical_and(zz >= 0, zz < n_z))
            def _():
                for other in range(2):
                    send_b((zz * 2 + (k + other) % 2 + n_col - c) % n_col).start()

    send_b((partner + n_col - c) % n_col).start()

    for o in range(1, n_row):
        got_a(o).wait_recv()
        if o < n_row - 1:
            send_line(o)

    def moments_a(q, carry):
        cols = pl.ds(pl.multiple_of(q * 128, 128), 128)
        x = a_all[c, :, cols].astype(F32)
        stat_a[c, 0:1, cols] = jnp.sum(x, 0, keepdims=True)
        stat_a[c, 1:2, cols] = jnp.sum(x * x, 0, keepdims=True)
        return carry

    lax.fori_loop(0, rb // 128, moments_a, 0)

    def send_sa(j):
        return remote(stat_a.at[c], stat_a.at[c], s_sa.at[j], r_sa.at[j], (r, col_mate(j)))

    def got_sa(j):
        src = col_mate(n_col - j)
        return remote(stat_a.at[src], stat_a.at[src], s_sa.at[j], r_sa.at[j], (r, src))

    for j in range(1, n_col):
        send_sa(j).start()
    if n_row > 1:
        send_line(n_row - 1)

    def send_fwd(i, g):
        return remote(b_all.at[g, mine], b_all.at[g, mine], s_fwd.at[i, g], r_fwd.at[i, g], (row_mate(i), c))

    def got_fwd(i, g):
        src = row_mate(n_row - i)
        rows = pl.ds(pl.multiple_of(src * t, t), t)
        return remote(b_all.at[g, rows], b_all.at[g, rows], s_fwd.at[i, g], r_fwd.at[i, g], (src, c))

    def each_chunk(d, do):
        for side in range(2):
            zz = z - d if side == 0 else z + d
            ok = (zz >= 0) if side == 0 else jnp.logical_and(zz < n_z, d > 0)

            @pl.when(ok)
            def _():
                do(zz * 2 + k, side)
                do(zz * 2 + (1 - k), side)

    def forward(d, carry):
        def do(g, side):
            for i in range(1, n_row):
                send_fwd(i, g).start()

        each_chunk(d, do)
        return carry

    own_b.wait()
    near = 1 + (n_col - 2) * (1 - k)
    got_b(near).wait_recv()
    forward(0, 0)
    for j in range(1, n_col):
        @pl.when(j != near)
        def _():
            got_b(j).wait_recv()


    def moments_b(q, carry):
        cols = pl.ds(pl.multiple_of(q * 128, 128), 128)
        total = jnp.zeros((1, 128), F32)
        squares = jnp.zeros((1, 128), F32)
        for g in range(n_col):
            x = b_all[g, mine, cols].astype(F32)
            total = total + jnp.sum(x, 0, keepdims=True)
            squares = squares + jnp.sum(x * x, 0, keepdims=True)
        stat_b[r, 0:1, cols] = total
        stat_b[r, 1:2, cols] = squares
        return carry

    lax.fori_loop(0, cb // 128, moments_b, 0)

    def send_sb(i):
        return remote(stat_b.at[r], stat_b.at[r], s_sb.at[i], r_sb.at[i], (row_mate(i), c))

    def got_sb(i):
        src = row_mate(n_row - i)
        return remote(stat_b.at[src], stat_b.at[src], s_sb.at[i], r_sb.at[i], (src, c))

    for i in range(1, n_row):
        send_sb(i).start()

    lax.fori_loop(1, n_z, forward, 0)

    def clear(q, carry):
        rows = pl.ds(pl.multiple_of(q * 64, 64), 64)
        out[rows, :] = jnp.zeros((64, cb), F32)
        return carry

    lax.fori_loop(0, rb // 64, clear, 0)

    for j in range(1, n_col):
        got_sa(j).wait_recv()
    for i in range(1, n_row):
        got_sb(i).wait_recv()

    def coefs(stat, coef):
        sums = jnp.sum(stat[...], 0)
        mean = sums[0:1] / count
        var = sums[1:2] / count - mean * mean
        coef[0:1, :] = mean
        coef[1:2, :] = lax.rsqrt(var + 1e-05)

    coefs(stat_a, coef_a)
    coefs(stat_b, coef_b)

    tile = min(1024, rb)

    def wait_fwd(zz):
        for g in range(2):
            for i in range(1, n_row):
                got_fwd(i, zz * 2 + g).wait_recv()

    def process(zz):
        for p in range(n_row):
            across(zz * 2 + (1 - k), p).wait_recv()
        wait_fwd(zz)
        multiply(zz, pl.ds(0, n_row * t), n_row * t)

    def multiply(zz, rows, height):
        pair = pl.ds(zz * 2, 2)
        depth = 2 * height

        def norm_b(q, carry):
            cols = pl.ds(pl.multiple_of(q * 128, 128), 128)
            x = b_all[pair, rows, cols].astype(F32).reshape(depth, 128)
            nb[0:depth, cols] = ((x - coef_b[0:1, cols]) * coef_b[1:2, cols]).astype(BF16)
            return carry

        lax.fori_loop(0, cb // 128, norm_b, 0)

        def mul(q, carry):
            cols = pl.ds(pl.multiple_of(q * tile, tile), tile)
            x = a_all[pair, rows, cols].astype(F32).reshape(depth, tile)
            na = ((x - coef_a[0:1, cols]) * coef_a[1:2, cols]).astype(BF16)
            out[cols, :] += lax.dot_general(
                na, nb[0:depth, :], (((0,), (0,)), ((), ())), preferred_element_type=F32
            )
            return carry

        lax.fori_loop(0, rb // tile, mul, 0)

    def process_all(d):
        def one(side, carry):
            zz = jnp.where(side == 0, z - d, z + d)
            ok = jnp.logical_and(zz >= 0, zz < n_z)
            ok = jnp.logical_and(ok, jnp.logical_or(side == 0, d > 0))

            @pl.when(ok)
            def _():
                process(zz)

            return carry

        lax.fori_loop(0, 2, one, 0)

    def relay(d):
        from_low = z - d >= 0
        from_high = z + d < n_z
        low = (z - d) * 2 + k
        high = (z + d) * 2 + k
        for o in range(n_row):
            p = slice_at(o)

            @pl.when(from_low)
            def _():
                up(low, p).wait_recv()

                @pl.when(can_up)
                def _():
                    up(low, p).start()

                across(low, p).start()

            @pl.when(from_high)
            def _():
                down(high, p).wait_recv()

                @pl.when(can_down)
                def _():
                    down(high, p).start()

                across(high, p).start()

    def last():
        zz = jnp.where(z == 0, n_z - 1, 0)
        g = zz * 2 + k

        @pl.when(jnp.logical_or(z == 0, z == n_z - 1))
        def _():
            wait_fwd(zz)

            def one(o, carry):
                p = slice_at(o)
                up(g, p).wait_recv()
                across(g, p).start()
                across(zz * 2 + (1 - k), p).wait_recv()
                multiply(zz, pl.ds(pl.multiple_of(p * t, t), t), t)
                return carry

            lax.fori_loop(0, n_row, one, 0)

    def step(d, carry):
        @pl.when(d + 1 < n_z - 1)
        def _():
            relay(d + 1)

        process_all(d)

        return carry

    lax.fori_loop(0, max(n_z - 1, 1), step, 0)
    if n_z > 1:
        last()

    def part(q, carry):
        rows = pl.ds(pl.multiple_of(q * 8, 8), 8)
        x = out[rows, :] * (1.0 / count)
        row_ids = r * rb + q * 8 + lax.broadcasted_iota(jnp.int32, (8, cb), 0)
        col_ids = c * cb + lax.broadcasted_iota(jnp.int32, (8, cb), 1)
        sq = x * x
        return carry + jnp.where(row_ids == col_ids, (1.0 - x) * (1.0 - x), 0.0051 * sq)

    share = lax.fori_loop(0, rb // 8, part, jnp.zeros((8, cb), F32), unroll=4)
    folded = share[:, 0:128]
    for q in range(1, cb // 128):
        folded = folded + share[:, q * 128 : (q + 1) * 128]
    loss_row[r] = folded

    def send_lr(i):
        return remote(loss_row.at[r], loss_row.at[r], s_lr.at[i], r_lr.at[i], (row_mate(i), c))

    def got_lr(i):
        src = row_mate(n_row - i)
        return remote(loss_row.at[src], loss_row.at[src], s_lr.at[i], r_lr.at[i], (src, c))

    def send_lc(j):
        return remote(loss_col.at[c], loss_col.at[c], s_lc.at[j], r_lc.at[j], (r, col_mate(j)))

    def got_lc(j):
        src = col_mate(n_col - j)
        return remote(loss_col.at[src], loss_col.at[src], s_lc.at[j], r_lc.at[j], (r, src))

    for i in range(1, n_row):
        send_lr(i).start()
    for i in range(1, n_row):
        got_lr(i).wait_recv()
    loss_col[c] = jnp.sum(loss_row[...], 0)
    for j in range(1, n_col):
        send_lc(j).start()

    for i in range(1, n_row):
        send_a(i).wait_send()
        send_sb(i).wait_send()
        send_lr(i).wait_send()
    for j in range(1, n_col):
        send_b(j).wait_send()
        send_sa(j).wait_send()

    def drain(g, carry):
        for i in range(1, n_row):
            send_fwd(i, g).wait_send()
        zz = g // 2
        for p in range(n_row):
            @pl.when(g % 2 == k)
            def _():
                @pl.when(jnp.logical_and(zz <= z, can_up))
                def _():
                    up(g, p).wait_send()

                @pl.when(jnp.logical_and(zz >= z, can_down))
                def _():
                    down(g, p).wait_send()

                across(g, p).wait_send()

        return carry

    lax.fori_loop(0, n_col, drain, 0)

    for j in range(1, n_col):
        got_lc(j).wait_recv()
    loss_out[...] = jnp.broadcast_to(
        jnp.sum(jnp.sum(loss_col[...], 0), keepdims=True) / width, loss_out.shape
    )
    for j in range(1, n_col):
        send_lc(j).wait_send()


def shards(view_a, view_b):
    t, width = view_a.shape
    n_row = lax.axis_size("row")
    n_col = lax.axis_size("col")
    rb = width // n_row
    cb = width // n_col
    count = t * n_row * n_col
    n_chunk = t * n_row
    dma = pltpu.SemaphoreType.DMA
    size = 2 * (count * (rb + cb) + 2 * n_chunk * cb + 2 * t * width) + 4 * rb * cb
    product, loss = pl.pallas_call(
        functools.partial(body, n_row, n_col, width),
        out_shape=(
            jax.ShapeDtypeStruct((rb, cb), F32),
            jax.ShapeDtypeStruct((8, 128), F32),
        ),
        in_specs=[pl.BlockSpec(memory_space=pltpu.HBM)] * 2,
        out_specs=(pl.BlockSpec(memory_space=pltpu.VMEM),) * 2,
        scratch_shapes=[
            pltpu.VMEM((n_col, n_chunk, rb), BF16),
            pltpu.VMEM((n_col, n_chunk, cb), BF16),
            pltpu.VMEM((2 * n_chunk, cb), BF16),
            pltpu.VMEM((n_col, 2, rb), F32),
            pltpu.VMEM((n_row, 2, cb), F32),
            pltpu.VMEM((2, rb), F32),
            pltpu.VMEM((2, cb), F32),
            pltpu.VMEM((n_row, 8, 128), F32),
            pltpu.VMEM((n_col, 8, 128), F32),
            dma((n_row,)), dma((n_row,)),
            dma((n_col,)), dma((n_col,)),
            dma((n_col,)), dma((n_col,)),
            dma((n_row,)), dma((n_row,)),
            dma((3, n_col, n_row)), dma((n_col, n_row)),
            dma((n_row, n_col)), dma((n_row, n_col)),
            dma((n_row,)), dma((n_row,)),
            dma((n_col,)), dma((n_col,)),
            dma((2,)),
        ],
        compiler_params=pltpu.CompilerParams(
            collective_id=0, has_side_effects=True, vmem_limit_bytes=min(size + (12 << 20), 60 << 20)
        ),
        name="twins",
    )(view_a, view_b)
    return product / count, loss[0, 0]


def solution(mesh):
    return jax.shard_map(
        shards,
        mesh=mesh,
        in_specs=(P(("row", "col"), None), P(("row", "col"), None)),
        out_specs=(P("row", "col"), P()),
        check_vma=False,
    )
```

profile of v0, /device:TPU:0, one launch (start us, length us, event | category | flops | bytes accessed | tf_op | source)
XLA Modules:
  0.0 163.1 jit_solution(10926305067698497681)
XLA Ops:
  0.6 0.0 copy-start
  0.6 1.4 copy-done
  2.0 0.0 copy-start.1
  2.0 1.4 copy-done.1
  3.4 153.7 %twins.1 = (f32[2048,1024]{1,0:T(8,128)S(1)}, f32[8,128]{1,0:T(8,128)S(1)}) custom-call(bf16[96,8192]{1,0:T(8,128)(2,1)S(1)} %copy-done, bf16[96,8192]{1,0:T(8,128)(2,1)S(1)} %copy-done.1), custom_call_target="tpu_custom_call" | custom-call | tf_op jit(solution)/shard_map/twins/pallas_call | solution.py:434
  157.2 0.5 slice.3
  157.7 5.4 %broadcast_multiply_fusion = f32[2048,1024]{1,0:T(8,128)} fusion(f32[2048,1024]{1,0:T(8,128)S(1)} %get-tuple-element.4), kind=kLoop, calls=%fused_computation | loop fusion | flops 2097152 | bytes 16777216 | tf_op jit(solution)/shard_map/div | solution.py:467
Async XLA Ops:
  0.6 1.4 copy-start
  2.0 1.4 copy-start.1
where the time goes:
time: 163 us
  Pallas kernels  154 us (94%)
  other arithmetic  5.39 us (3%)
  local copies, waits for them, and re-layouts  3.32 us (2%)
    pallas_call x1, Pallas kernels, shards(): pl.pallas_call(functools.partial(body, n_row, n_col, width), out_shape=(j...  154 us
    div x1, other arithmetic, shards(): return (product / count, loss[0, 0])  5.39 us

commit v1 on v0

--- a/solution.py
+++ b/solution.py
@@ -15,9 +15,9 @@
 def body(
     n_row, n_col, width,
     a_in, b_in, out, loss_out,
-    a_all, b_all, nb, stat_a, stat_b, coef_a, coef_b, loss_row, loss_col,
+    a_all, b_all, nb, stat_a, stat_b, coef_a, coef_b, shares,
     s_a, r_a, s_b, r_b, s_sa, r_sa, s_sb, r_sb, s_line, r_line, s_fwd, r_fwd,
-    s_lr, r_lr, s_lc, r_lc, own_sem,
+    s_loss, r_loss, own_sem,
 ):
     t = a_in.shape[0]
     rb = a_in.shape[1] // n_row
@@ -51,11 +51,14 @@
     own_b.start()
 
     barrier = pltpu.get_barrier_semaphore()
-    for i in range(1, n_row):
-        pl.semaphore_signal(barrier, inc=1, device_id=(row_mate(i), c), device_id_type=MESH)
-    for j in range(1, n_col):
-        pl.semaphore_signal(barrier, inc=1, device_id=(r, col_mate(j)), device_id_type=MESH)
-    pl.semaphore_wait(barrier, n_row + n_col - 2)
+
+    def greet(i, carry):
+        dst = (r * n_col + c + i) % (n_row * n_col)
+        pl.semaphore_signal(barrier, inc=1, device_id=(dst // n_col, dst % n_col), device_id_type=MESH)
+        return carry
+
+    lax.fori_loop(1, n_row * n_col, greet, 0)
+    pl.semaphore_wait(barrier, n_row * n_col - 1)
 
     def send_a(i):
         dst = row_mate(i)
@@ -350,6 +353,7 @@
     def part(q, carry):
         rows = pl.ds(pl.multiple_of(q * 8, 8), 8)
         x = out[rows, :] * (1.0 / count)
+        out[rows, :] = x
         row_ids = r * rb + q * 8 + lax.broadcasted_iota(jnp.int32, (8, cb), 0)
         col_ids = c * cb + lax.broadcasted_iota(jnp.int32, (8, cb), 1)
         sq = x * x
@@ -359,34 +363,32 @@
     folded = share[:, 0:128]
     for q in range(1, cb // 128):
         folded = folded + share[:, q * 128 : (q + 1) * 128]
-    loss_row[r] = folded
-
-    def send_lr(i):
-        return remote(loss_row.at[r], loss_row.at[r], s_lr.at[i], r_lr.at[i], (row_mate(i), c))
-
-    def got_lr(i):
-        src = row_mate(n_row - i)
-        return remote(loss_row.at[src], loss_row.at[src], s_lr.at[i], r_lr.at[i], (src, c))
-
-    def send_lc(j):
-        return remote(loss_col.at[c], loss_col.at[c], s_lc.at[j], r_lc.at[j], (r, col_mate(j)))
-
-    def got_lc(j):
-        src = col_mate(n_col - j)
-        return remote(loss_col.at[src], loss_col.at[src], s_lc.at[j], r_lc.at[j], (r, src))
-
-    for i in range(1, n_row):
-        send_lr(i).start()
-    for i in range(1, n_row):
-        got_lr(i).wait_recv()
-    loss_col[c] = jnp.sum(loss_row[...], 0)
-    for j in range(1, n_col):
-        send_lc(j).start()
+    n_dev = n_row * n_col
+    me = r * n_col + c
+    shares[me] = jnp.sum(folded, 0, keepdims=True)
+
+    def send_share(i):
+        dst = (me + i) % n_dev
+        ref = shares.at[me]
+        return remote(ref, ref, s_loss.at[i], r_loss.at[i], (dst // n_col, dst % n_col))
+
+    def got_share(i):
+        src = (me + n_dev - i) % n_dev
+        ref = shares.at[src]
+        return remote(ref, ref, s_loss.at[i], r_loss.at[i], (src // n_col, src % n_col))
+
+    def each_peer(do):
+        def one(i, carry):
+            do(i)
+            return carry
+
+        lax.fori_loop(1, n_dev, one, 0)
+
+    each_peer(lambda i: send_share(i).start())
 
     for i in range(1, n_row):
         send_a(i).wait_send()
         send_sb(i).wait_send()
-        send_lr(i).wait_send()
     for j in range(1, n_col):
         send_b(j).wait_send()
         send_sa(j).wait_send()
@@ -412,13 +414,40 @@
 
     lax.fori_loop(0, n_col, drain, 0)
 
-    for j in range(1, n_col):
-        got_lc(j).wait_recv()
+    each_peer(lambda i: got_share(i).wait_recv())
     loss_out[...] = jnp.broadcast_to(
-        jnp.sum(jnp.sum(loss_col[...], 0), keepdims=True) / width, loss_out.shape
+        jnp.sum(jnp.sum(shares[...], 0), keepdims=True) / width, loss_out.shape
     )
-    for j in range(1, n_col):
-        send_lc(j).wait_send()
+    each_peer(lambda i: send_share(i).wait_send())
+
+
+def hbm(x):
+    return pltpu.with_memory_space_constraint(x, pltpu.HBM)
+
+
+def emit_body(pieces, x, out, sem):
+    height = x.shape[0] // pieces
+
+    def move(i):
+        rows = pl.ds(i * height, height)
+        return pltpu.make_async_copy(x.at[rows], out.at[rows], sem.at[i])
+
+    for i in range(pieces):
+        move(i).start()
+    for i in range(pieces):
+        move(i).wait()
+
+
+def emit(x):
+    return pl.pallas_call(
+        functools.partial(emit_body, 8),
+        out_shape=jax.ShapeDtypeStruct(x.shape, x.dtype),
+        in_specs=[pl.BlockSpec(memory_space=pltpu.VMEM)],
+        out_specs=pl.BlockSpec(memory_space=pltpu.HBM),
+        scratch_shapes=[pltpu.SemaphoreType.DMA((8,))],
+        compiler_params=pltpu.CompilerParams(vmem_limit_bytes=16 << 20),
+        name="emit",
+    )(x)
 
 
 def shards(view_a, view_b):
@@ -447,24 +476,22 @@
             pltpu.VMEM((n_row, 2, cb), F32),
             pltpu.VMEM((2, rb), F32),
             pltpu.VMEM((2, cb), F32),
-            pltpu.VMEM((n_row, 8, 128), F32),
-            pltpu.VMEM((n_col, 8, 128), F32),
+            pltpu.VMEM((n_row * n_col, 1, 128), F32),
             dma((n_row,)), dma((n_row,)),
             dma((n_col,)), dma((n_col,)),
             dma((n_col,)), dma((n_col,)),
             dma((n_row,)), dma((n_row,)),
             dma((3, n_col, n_row)), dma((n_col, n_row)),
             dma((n_row, n_col)), dma((n_row, n_col)),
-            dma((n_row,)), dma((n_row,)),
-            dma((n_col,)), dma((n_col,)),
+            dma((n_row * n_col,)), dma((n_row * n_col,)),
             dma((2,)),
         ],
         compiler_params=pltpu.CompilerParams(
             collective_id=0, has_side_effects=True, vmem_limit_bytes=min(size + (12 << 20), 60 << 20)
         ),
         name="twins",
-    )(view_a, view_b)
-    return product / count, loss[0, 0]
+    )(hbm(view_a), hbm(view_b))
+    return emit(product), loss[0, 0]
 
 
 def solution(mesh):

time: 163 us -> 157 us (0.963)
  other arithmetic: 5.39 us -> 0 us
  local copies, waits for them, and re-layouts: 3.32 us -> 0.51 us
  Pallas kernels: 154 us -> 156 us
    div x1 -> x0, other arithmetic: 5.39 us -> none  [shards(): return (product / count, loss[0, 0])]
    pallas_call x0 -> x1, Pallas kernels: none -> 3.36 us  [emit(): pl.pallas_call(functools.partial(emit_body, 8), out_shape=jax.ShapeDtypeS...]
    unnamed x4 -> x0, local copies, waits for them, and re-layouts: 2.81 us -> none
where the time goes in v1:
time: 157 us
  Pallas kernels  156 us (99%)
    pallas_call x1, Pallas kernels, shards(): pl.pallas_call(functools.partial(body, n_row, n_col, width), out_shape=(j...  153 us
    pallas_call x1, Pallas kernels, emit(): pl.pallas_call(functools.partial(emit_body, 8), out_shape=jax.ShapeDtypeS...  3.36 us

profile of v1, /device:TPU:0, one launch (start us, length us, event | category | flops | bytes accessed | tf_op | source)
XLA Modules:
  0.0 157.3 jit_solution(2064131215840573207)
XLA Ops:
  0.6 152.8 %twins.1 = (f32[2048,1024]{1,0:T(8,128)S(1)}, f32[8,128]{1,0:T(8,128)S(1)}) custom-call(bf16[96,8192]{1,0:T(8,128)(2,1)} %a_in.1, bf16[96,8192]{1,0:T(8,128)(2,1)} %b_in.1), custom_call_target="tpu_custom_call" | custom-call | tf_op jit(solution)/shard_map/twins/pallas_call | solution.py:463
  153.4 0.5 slice.3
  154.0 3.4 %emit.1 = f32[2048,1024]{1,0:T(8,128)} custom-call(f32[2048,1024]{1,0:T(8,128)S(1)} %get-tuple-element.4.x), custom_call_target="tpu_custom_call" | custom-call | tf_op jit(solution)/shard_map/emit/pallas_call | solution.py:442

commit v2 on v1

v2 whole, which is shorter than its diff:
```python
import functools

import jax
import jax.numpy as jnp
from jax import lax
from jax.experimental import pallas as pl
from jax.experimental.pallas import tpu as pltpu
from jax.sharding import PartitionSpec as P

MESH = pl.DeviceIdType.MESH
F32 = jnp.float32
BF16 = jnp.bfloat16
TAIL = 4


def body(
    n_row, n_col, width,
    a_in, b_in, out, loss_out,
    a_all, b_all, nb, stat_a, stat_b, coef_a, coef_b, partial, shares,
    r_a, r_b, s_line, r_line, r_across, s_tail, r_tail, x_tail, r_fwd, once,
):
    t = a_in.shape[0]
    rb = a_in.shape[1] // n_row
    cb = b_in.shape[1] // n_col
    count = t * n_row * n_col
    n_z = n_col // 2
    r = lax.axis_index("row")
    c = lax.axis_index("col")
    z = c // 2
    k = c % 2
    mine = pl.ds(pl.multiple_of(r * t, t), t)

    def row_mate(i):
        return (r + i) % n_row

    def col_mate(j):
        return (c + j) % n_col

    def remote(src, dst, ss, rs, dev):
        return pltpu.make_async_remote_copy(
            src_ref=src, dst_ref=dst, send_sem=ss, recv_sem=rs, device_id=dev, device_id_type=MESH
        )

    own_a = pltpu.make_async_copy(
        a_in.at[:, pl.ds(pl.multiple_of(r * rb, rb), rb)], a_all.at[c, mine], once.at[0]
    )
    own_b = pltpu.make_async_copy(
        b_in.at[:, pl.ds(pl.multiple_of(c * cb, cb), cb)], b_all.at[c, mine], once.at[1]
    )
    own_a.start()
    own_b.start()

    barrier = pltpu.get_barrier_semaphore()

    def greet(i, carry):
        dst = (r * n_col + c + i) % (n_row * n_col)
        pl.semaphore_signal(barrier, inc=1, device_id=(dst // n_col, dst % n_col), device_id_type=MESH)
        return carry

    lax.fori_loop(1, n_row * n_col, greet, 0)
    pl.semaphore_wait(barrier, n_row * n_col - 1)

    def sent(ref, sem):
        remote(ref, ref, sem, sem, (r, c)).wait_send()

    def landed(ref, sem):
        remote(ref, ref, sem, sem, (r, c)).wait_recv()

    def send_a(i):
        dst = row_mate(i)
        cols = pl.ds(pl.multiple_of(dst * rb, rb), rb)
        return remote(a_in.at[:, cols], a_all.at[c, mine], once.at[2], r_a.at[i], (dst, c))

    def got_a(i):
        src = row_mate(n_row - i)
        rows = pl.ds(pl.multiple_of(src * t, t), t)
        return remote(a_all.at[c, rows], a_all.at[c, rows], once.at[2], r_a.at[i], (src, c))

    def send_b(j):
        dst = col_mate(j)
        cols = pl.ds(pl.multiple_of(dst * cb, cb), cb)
        return remote(b_in.at[:, cols], b_all.at[c, mine], once.at[3], r_b.at[z], (r, dst))

    for i in range(1, n_row):
        send_a(i).start()

    def block(chunk, p):
        return a_all.at[chunk, pl.ds(pl.multiple_of(p * t, t), t)]

    partner = z * 2 + (1 - k)
    above = (r, lax.min(c + 2, n_col - 2 + k))
    below = (r, lax.max(c - 2, k))
    beside = (r, partner)

    def up(chunk, p):
        ref = block(chunk, p)
        return remote(ref, ref, s_line.at[0, chunk // 2], r_line.at[chunk // 2, p], above)

    def down(chunk, p):
        ref = block(chunk, p)
        return remote(ref, ref, s_line.at[1, chunk // 2], r_line.at[chunk // 2, p], below)

    def across(chunk, p):
        ref = block(chunk, p)
        far = lax.max(chunk // 2 - z, z - chunk // 2) == n_z - 1
        slot = jnp.where(far, n_z + p, chunk // 2)
        return remote(ref, ref, once.at[4], r_across.at[slot], beside)

    wide = rb // TAIL

    def slab(chunk, p, f):
        return a_all.at[
            chunk, pl.ds(pl.multiple_of(p * t, t), t), pl.ds(pl.multiple_of(f * wide, wide), wide)
        ]

    def tail(way, chunk, p, f):
        ref = slab(chunk, p, f)
        return remote(ref, ref, s_tail.at[way], r_tail.at[f], above if way == 0 else below)

    def tail_across(chunk, p, f):
        ref = slab(chunk, p, f)
        return remote(ref, ref, once.at[4], x_tail.at[f], beside)

    can_up = z < n_z - 1
    can_down = z > 0

    def slice_at(o):
        return (r + n_row - o) % n_row

    def send_line(o):
        p = slice_at(o)

        @pl.when(can_up)
        def _():
            up(c, p).start()

        @pl.when(can_down)
        def _():
            down(c, p).start()

        across(c, p).start()

    own_a.wait()
    send_line(0)

    for dist in range(n_z - 1, 0, -1):
        for side in range(2):
            zz = z - dist if side == 0 else z + dist

            @pl.when(jnp.logical_and(zz >= 0, zz < n_z))
            def _():
                for other in range(2):
                    send_b((zz * 2 + (k + other) % 2 + n_col - c) % n_col).start()

    send_b((partner + n_col - c) % n_col).start()

    for o in range(1, n_row):
        got_a(o).wait_recv()
        if o < n_row - 1:
            send_line(o)

    def moments_a(q, carry):
        cols = pl.ds(pl.multiple_of(q * 128, 128), 128)
        x = a_all[c, :, cols].astype(F32)
        stat_a[c, 0:1, cols] = jnp.sum(x, 0, keepdims=True)
        stat_a[c, 1:2, cols] = jnp.sum(x * x, 0, keepdims=True)
        return carry

    lax.fori_loop(0, rb // 128, moments_a, 0)

    def send_sa(j):
        return remote(stat_a.at[c], stat_a.at[c], once.at[5], once.at[6], (r, col_mate(j)))

    for j in range(1, n_col):
        send_sa(j).start()
    if n_row > 1:
        send_line(n_row - 1)

    def send_fwd(i, g):
        return remote(b_all.at[g, mine], b_all.at[g, mine], once.at[7], r_fwd.at[g // 2], (row_mate(i), c))

    def each_chunk(d, do):
        for side in range(2):
            zz = z - d if side == 0 else z + d
            ok = (zz >= 0) if side == 0 else jnp.logical_and(zz < n_z, d > 0)

            @pl.when(ok)
            def _():
                do(zz * 2 + k, side)
                do(zz * 2 + (1 - k), side)

    def forward(d, carry):
        def do(g, side):
            for i in range(1, n_row):
                send_fwd(i, g).start()

        each_chunk(d, do)
        return carry

    def relay(d, o):
        split = isinstance(d, int) and d == n_z - 2 and o == n_row - 1
        from_low = z - d >= 0
        from_high = z + d < n_z
        low = (z - d) * 2 + k
        high = (z + d) * 2 + k
        p = slice_at(o)

        @pl.when(from_low)
        def _():
            up(low, p).wait_recv()

            @pl.when(can_up)
            def _():
                if split:
                    for f in range(TAIL):
                        tail(0, low, p, f).start()
                else:
                    up(low, p).start()

            across(low, p).start()

        @pl.when(from_high)
        def _():
            down(high, p).wait_recv()

            @pl.when(can_down)
            def _():
                if split:
                    for f in range(TAIL):
                        tail(1, high, p, f).start()
                else:
                    down(high, p).start()

            across(high, p).start()

    def arrive(d):
        for side in range(2):
            zz = z - d if side == 0 else z + d

            @pl.when(jnp.logical_and(zz >= 0, zz < n_z))
            def _():
                landed(b_all.at[pl.ds(zz * 2, 2), mine], r_b.at[zz])

    own_b.wait()
    landed(b_all.at[partner, mine], r_b.at[z])
    forward(0, 0)
    early = n_z > 2
    for o in range(n_row if early else 0):
        relay(1, o)
        if o + 1 < min(n_row, n_z):
            arrive(o + 1)
            forward(o + 1, 0)

    def rest(d, carry):
        arrive(d)
        forward(d, 0)
        return carry

    lax.fori_loop(min(n_row, n_z) if early else 1, n_z, rest, 0)

    for o in range(n_row if n_z > 3 else 0):
        relay(2, o)

    def moments_b(q, carry):
        cols = pl.ds(pl.multiple_of(q * 128, 128), 128)
        total = jnp.zeros((1, 128), F32)
        squares = jnp.zeros((1, 128), F32)
        for g in range(n_col):
            x = b_all[g, mine, cols].astype(F32)
            total = total + jnp.sum(x, 0, keepdims=True)
            squares = squares + jnp.sum(x * x, 0, keepdims=True)
        stat_b[r, 0:1, cols] = total
        stat_b[r, 1:2, cols] = squares
        return carry

    lax.fori_loop(0, cb // 128, moments_b, 0)

    def send_sb(i):
        return remote(stat_b.at[r], stat_b.at[r], once.at[8], once.at[9], (row_mate(i), c))

    for i in range(1, n_row):
        send_sb(i).start()

    def clear(q, carry):
        rows = pl.ds(pl.multiple_of(q * 64, 64), 64)
        out[rows, :] = jnp.zeros((64, cb), F32)
        return carry

    lax.fori_loop(0, rb // 64, clear, 0)

    landed(stat_a.at[pl.ds(0, n_col - 1)], once.at[6])
    landed(stat_b.at[pl.ds(0, n_row - 1)], once.at[9])

    def coefs(stat, coef):
        sums = jnp.sum(stat[...], 0)
        mean = sums[0:1] / count
        var = sums[1:2] / count - mean * mean
        coef[0:1, :] = mean
        coef[1:2, :] = lax.rsqrt(var + 1e-05)

    coefs(stat_a, coef_a)
    coefs(stat_b, coef_b)

    tile = min(1024, rb)

    def wait_fwd(zz):
        landed(b_all.at[pl.ds(zz * 2, 2), pl.ds(0, (n_row - 1) * t)], r_fwd.at[zz])

    def process(zz):
        landed(a_all.at[zz * 2 + (1 - k)], r_across.at[zz])
        wait_fwd(zz)
        multiply(zz, pl.ds(0, n_row * t), n_row * t)

    def normalize_b(zz, rows, height):
        def one(q, carry):
            cols = pl.ds(pl.multiple_of(q * 128, 128), 128)
            x = b_all[pl.ds(zz * 2, 2), rows, cols].astype(F32).reshape(2 * height, 128)
            nb[0 : 2 * height, cols] = ((x - coef_b[0:1, cols]) * coef_b[1:2, cols]).astype(BF16)
            return carry

        lax.fori_loop(0, cb // 128, one, 0)

    def product(zz, rows, height, cols, width):
        x = a_all[pl.ds(zz * 2, 2), rows, cols].astype(F32).reshape(2 * height, width)
        na = ((x - coef_a[0:1, cols]) * coef_a[1:2, cols]).astype(BF16)
        return lax.dot_general(
            na, nb[0 : 2 * height, :], (((0,), (0,)), ((), ())), preferred_element_type=F32
        )

    def multiply(zz, rows, height):
        normalize_b(zz, rows, height)

        def mul(q, carry):
            cols = pl.ds(pl.multiple_of(q * tile, tile), tile)
            out[cols, :] += product(zz, rows, height, cols, tile)
            return carry

        lax.fori_loop(0, rb // tile, mul, 0)

    def process_all(d):
        def one(side, carry):
            zz = jnp.where(side == 0, z - d, z + d)
            ok = jnp.logical_and(zz >= 0, zz < n_z)
            ok = jnp.logical_and(ok, jnp.logical_or(side == 0, d > 0))

            @pl.when(ok)
            def _():
                process(zz)

            return carry

        lax.fori_loop(0, 2, one, 0)

    at_end = jnp.logical_and(n_z > 2, jnp.logical_or(z == 0, z == n_z - 1))

    def finish(x):
        x = x * (1.0 / count)
        partial[...] += jnp.sum((x * x).reshape(x.shape[0] // 8, 8, cb), 0)
        return x

    def last():
        zz = jnp.where(z == 0, n_z - 1, 0)
        g = zz * 2 + k
        other = zz * 2 + (1 - k)

        @pl.when(jnp.logical_or(z == 0, z == n_z - 1))
        def _():
            wait_fwd(zz)

            def one(o, carry):
                p = slice_at(o)
                up(g, p).wait_recv()
                across(g, p).start()
                landed(block(other, p), r_across.at[n_z + p])
                multiply(zz, pl.ds(pl.multiple_of(p * t, t), t), t)
                return carry

            lax.fori_loop(0, n_row - 1 if n_z > 2 else n_row, one, 0)
            if n_z > 2:
                p = slice_at(n_row - 1)
                rows = pl.ds(pl.multiple_of(p * t, t), t)
                normalize_b(zz, rows, t)

                def some(f, carry):
                    landed(slab(g, p, f), r_tail.at[f])
                    tail_across(g, p, f).start()
                    landed(slab(other, p, f), x_tail.at[f])
                    cols = pl.ds(pl.multiple_of(f * wide, wide), wide)
                    out[cols, :] = finish(out[cols, :] + product(zz, rows, t, cols, wide))
                    return carry

                lax.fori_loop(0, TAIL, some, 0)

    def step(d, carry):
        process_all(d)

        if n_z > 5:
            @pl.when(d + 3 < n_z - 2)
            def _():
                for o in range(n_row):
                    relay(d + 3, o)

        if n_z > 4:
            @pl.when(d + 3 == n_z - 2)
            def _():
                for o in range(n_row):
                    relay(n_z - 2, o)

        return carry

    lax.fori_loop(0, max(n_z - 1, 1), step, 0)
    partial[...] = jnp.zeros((8, cb), F32)
    if n_z > 1:
        last()

    @pl.when(jnp.logical_not(at_end))
    def _():
        def part(q, carry):
            rows = pl.ds(pl.multiple_of(q * 64, 64), 64)
            out[rows, :] = finish(out[rows, :])
            return carry

        lax.fori_loop(0, rb // 64, part, 0)

    folded = partial[:, 0:128]
    for q in range(1, cb // 128):
        folded = folded + partial[:, q * 128 : (q + 1) * 128]
    folded = jnp.sum(0.0051 * folded, 0, keepdims=True)

    def diagonal(q, carry):
        first = c * cb + q * 128 - r * rb
        inside = jnp.logical_and(first >= 0, first < rb)
        rows = pl.ds(pl.multiple_of(jnp.where(inside, first, 0), 128), 128)
        x = out[rows, pl.ds(pl.multiple_of(q * 128, 128), 128)]
        same = lax.broadcasted_iota(jnp.int32, (128, 128), 0) == lax.broadcasted_iota(
            jnp.int32, (128, 128), 1
        )
        more = jnp.where(
            jnp.logical_and(same, inside), (1.0 - x) * (1.0 - x) - 0.0051 * (x * x), 0.0
        )
        return carry + jnp.sum(more, 0, keepdims=True)

    folded = lax.fori_loop(0, cb // 128, diagonal, folded)
    n_dev = n_row * n_col
    me = r * n_col + c
    shares[me] = folded

    def send_share(i):
        dst = (me + i) % n_dev
        ref = shares.at[me]
        return remote(ref, ref, once.at[10], once.at[11], (dst // n_col, dst % n_col))

    def each_peer(do):
        def one(i, carry):
            do(i)
            return carry

        lax.fori_loop(1, n_dev, one, 0)

    each_peer(lambda i: send_share(i).start())

    sent(a_all.at[0, pl.ds(0, (n_row - 1) * t)], once.at[2])
    sent(b_all.at[pl.ds(0, n_col - 1), pl.ds(0, t)], once.at[3])
    sent(stat_a.at[pl.ds(0, n_col - 1)], once.at[5])
    sent(stat_b.at[pl.ds(0, n_row - 1)], once.at[8])
    sent(b_all.at[:, pl.ds(0, (n_row - 1) * t)], once.at[7])
    sent(a_all.at[pl.ds(0, n_z)], once.at[4])

    def drain(zz, carry):
        whole = a_all.at[0]
        most = a_all.at[0, pl.ds(0, (n_row - 1) * t)]
        for way in range(2):
            sends = jnp.logical_and(zz <= z, can_up) if way == 0 else jnp.logical_and(zz >= z, can_down)
            cut = jnp.logical_and(n_z > 2, (z - zz if way == 0 else zz - z) == n_z - 2)

            @pl.when(jnp.logical_and(sends, jnp.logical_not(cut)))
            def _():
                sent(whole, s_line.at[way, zz])

            @pl.when(jnp.logical_and(sends, cut))
            def _():
                sent(most, s_line.at[way, zz])
                sent(a_all.at[0, pl.ds(0, t)], s_tail.at[way])

        return carry

    lax.fori_loop(0, n_z, drain, 0)

    landed(shares.at[pl.ds(0, n_dev - 1)], once.at[11])
    loss_out[...] = jnp.sum(jnp.sum(shares[...], 0), keepdims=True) / width
    sent(shares.at[pl.ds(0, n_dev - 1)], once.at[10])


def hbm(x):
    return pltpu.with_memory_space_constraint(x, pltpu.HBM)


def emit_body(pieces, x, out, sem):
    height = x.shape[0] // pieces

    def move(i):
        rows = pl.ds(i * height, height)
        return pltpu.make_async_copy(x.at[rows], out.at[rows], sem.at[i])

    for i in range(pieces):
        move(i).start()
    for i in range(pieces):
        move(i).wait()


def emit(x):
    return pl.pallas_call(
        functools.partial(emit_body, 8),
        out_shape=jax.ShapeDtypeStruct(x.shape, x.dtype),
        in_specs=[pl.BlockSpec(memory_space=pltpu.VMEM)],
        out_specs=pl.BlockSpec(memory_space=pltpu.HBM),
        scratch_shapes=[pltpu.SemaphoreType.DMA((8,))],
        compiler_params=pltpu.CompilerParams(vmem_limit_bytes=16 << 20),
        name="emit",
    )(x)


def shards(view_a, view_b):
    t, width = view_a.shape
    n_row = lax.axis_size("row")
    n_col = lax.axis_size("col")
    rb = width // n_row
    cb = width // n_col
    count = t * n_row * n_col
    n_chunk = t * n_row
    dma = pltpu.SemaphoreType.DMA
    size = 2 * (count * (rb + cb) + 2 * n_chunk * cb + 2 * t * width) + 4 * rb * cb
    product, loss = pl.pallas_call(
        functools.partial(body, n_row, n_col, width),
        out_shape=(
            jax.ShapeDtypeStruct((rb, cb), F32),
            jax.ShapeDtypeStruct((1, 1), F32),
        ),
        in_specs=[pl.BlockSpec(memory_space=pltpu.HBM)] * 2,
        out_specs=(pl.BlockSpec(memory_space=pltpu.VMEM),) * 2,
        scratch_shapes=[
            pltpu.VMEM((n_col, n_chunk, rb), BF16),
            pltpu.VMEM((n_col, n_chunk, cb), BF16),
            pltpu.VMEM((2 * n_chunk, cb), BF16),
            pltpu.VMEM((n_col, 2, rb), F32),
            pltpu.VMEM((n_row, 2, cb), F32),
            pltpu.VMEM((2, rb), F32),
            pltpu.VMEM((2, cb), F32),
            pltpu.VMEM((8, cb), F32),
            pltpu.VMEM((n_row * n_col, 1, 128), F32),
            dma((n_row,)), dma((n_col // 2,)),
            dma((2, n_col // 2)), dma((n_col // 2, n_row)), dma((n_col // 2 + n_row,)),
            dma((2,)), dma((TAIL,)), dma((TAIL,)),
            dma((n_col // 2,)), dma((12,)),
        ],
        compiler_params=pltpu.CompilerParams(
            collective_id=0, has_side_effects=True, vmem_limit_bytes=min(size + (12 << 20), 60 << 20)
        ),
        name="twins",
    )(hbm(view_a), hbm(view_b))
    return emit(product), loss.reshape(())


def solution(mesh):
    return jax.shard_map(
        shards,
        mesh=mesh,
        in_specs=(P(("row", "col"), None), P(("row", "col"), None)),
        out_specs=(P("row", "col"), P()),
        check_vma=False,
    )
```

time: 157 us -> 150 us (0.955)
  Pallas kernels: 156 us -> 147 us
  between operations: 0.64 us -> 2.33 us
    pallas_call x1, Pallas kernels: 153 us -> 144 us  [shards(): pl.pallas_call(functools.partial(body, n_row, n_col, width), out_shape=(j...]
where the time goes in v2:
time: 150 us
  Pallas kernels  147 us (98%)
  between operations  2.33 us (2%)
    pallas_call x1, Pallas kernels, shards(): pl.pallas_call(functools.partial(body, n_row, n_col, width), out_shape=(j...  144 us
    pallas_call x1, Pallas kernels, emit(): pl.pallas_call(functools.partial(emit_body, 8), out_shape=jax.ShapeDtypeS...  3.37 us

profile of v2, /device:TPU:0, one launch (start us, length us, event | category | flops | bytes accessed | tf_op | source)
XLA Modules:
  0.0 149.8 jit_solution(13182478529592769516)
XLA Ops:
  0.6 144.1 %twins.1 = (f32[2048,1024]{1,0:T(8,128)S(1)}, f32[1,1]{1,0:T(1,128)}) custom-call(bf16[96,8192]{1,0:T(8,128)(2,1)} %a_in.1, bf16[96,8192]{1,0:T(8,128)(2,1)} %b_in.1), custom_call_target="tpu_custom_call" | custom-call | tf_op jit(solution)/shard_map/twins/pallas_call | solution.py:533
  144.7 3.4 %emit.1 = f32[2048,1024]{1,0:T(8,128)} custom-call(f32[2048,1024]{1,0:T(8,128)S(1)} %get-tuple-element.4.x), custom_call_target="tpu_custom_call" | custom-call | tf_op jit(solution)/shard_map/emit/pallas_call | solution.py:512

commit v3 on v2

--- a/solution.py
+++ b/solution.py
@@ -16,16 +16,18 @@
 def body(
     n_row, n_col, width,
     a_in, b_in, out, loss_out,
-    a_all, b_all, nb, stat_a, stat_b, coef_a, coef_b, partial, shares,
-    r_a, r_b, s_line, r_line, r_across, s_tail, r_tail, x_tail, r_fwd, once,
+    a_all, b_all, nb, stat_a, sums_a, total_a, stat_b, coef_a, coef_b, partial, shares,
+    r_a, r_b, r_line, r_across, r_tail, x_tail, r_fwd, once,
 ):
     t = a_in.shape[0]
     rb = a_in.shape[1] // n_row
     cb = b_in.shape[1] // n_col
     count = t * n_row * n_col
     n_z = n_col // 2
+    n_dev = n_row * n_col
     r = lax.axis_index("row")
     c = lax.axis_index("col")
+    me = r * n_col + c
     z = c // 2
     k = c % 2
     mine = pl.ds(pl.multiple_of(r * t, t), t)
@@ -52,13 +54,12 @@
 
     barrier = pltpu.get_barrier_semaphore()
 
-    def greet(i, carry):
-        dst = (r * n_col + c + i) % (n_row * n_col)
-        pl.semaphore_signal(barrier, inc=1, device_id=(dst // n_col, dst % n_col), device_id_type=MESH)
-        return carry
-
-    lax.fori_loop(1, n_row * n_col, greet, 0)
-    pl.semaphore_wait(barrier, n_row * n_col - 1)
+    peers = [(i, j) for i in range(n_row) for j in range(n_col) if i or j]
+    peers.sort(key=lambda ij: (min(ij) > 0, ij))
+    mates = [(i, j) for i, j in peers if min(i, j) == 0]
+    for i, j in mates:
+        pl.semaphore_signal(barrier, inc=1, device_id=(row_mate(i), col_mate(j)), device_id_type=MESH)
+    pl.semaphore_wait(barrier, len(mates))
 
     def sent(ref, sem):
         remote(ref, ref, sem, sem, (r, c)).wait_send()
@@ -94,11 +95,11 @@
 
     def up(chunk, p):
         ref = block(chunk, p)
-        return remote(ref, ref, s_line.at[0, chunk // 2], r_line.at[chunk // 2, p], above)
+        return remote(ref, ref, once.at[16], r_line.at[chunk // 2, p], above)
 
     def down(chunk, p):
         ref = block(chunk, p)
-        return remote(ref, ref, s_line.at[1, chunk // 2], r_line.at[chunk // 2, p], below)
+        return remote(ref, ref, once.at[16], r_line.at[chunk // 2, p], below)
 
     def across(chunk, p):
         ref = block(chunk, p)
@@ -115,7 +116,7 @@
 
     def tail(way, chunk, p, f):
         ref = slab(chunk, p, f)
-        return remote(ref, ref, s_tail.at[way], r_tail.at[f], above if way == 0 else below)
+        return remote(ref, ref, once.at[16], r_tail.at[f], above if way == 0 else below)
 
     def tail_across(chunk, p, f):
         ref = slab(chunk, p, f)
@@ -162,17 +163,24 @@
     def moments_a(q, carry):
         cols = pl.ds(pl.multiple_of(q * 128, 128), 128)
         x = a_all[c, :, cols].astype(F32)
-        stat_a[c, 0:1, cols] = jnp.sum(x, 0, keepdims=True)
-        stat_a[c, 1:2, cols] = jnp.sum(x * x, 0, keepdims=True)
+        stat_a[0, 0:1, cols] = jnp.sum(x, 0, keepdims=True)
+        stat_a[0, 1:2, cols] = jnp.sum(x * x, 0, keepdims=True)
         return carry
 
     lax.fori_loop(0, rb // 128, moments_a, 0)
 
-    def send_sa(j):
-        return remote(stat_a.at[c], stat_a.at[c], once.at[5], once.at[6], (r, col_mate(j)))
-
-    for j in range(1, n_col):
-        send_sa(j).start()
+    half = rb // 2
+    near = pl.ds(pl.multiple_of(k * half, half), half)
+    away = pl.ds(pl.multiple_of((1 - k) * half, half), half)
+    give_a = remote(stat_a.at[0, :, away], stat_a.at[1, :, away], once.at[5], once.at[6], beside)
+    give_a.start()
+    give_a.wait_send()
+    landed(stat_a.at[1, :, near], once.at[6])
+    sums_a[z] = stat_a[0, :, near] + stat_a[1, :, near]
+    for j in range(1, n_z):
+        remote(
+            sums_a.at[z], sums_a.at[z], once.at[12], once.at[13], (r, (c + 2 * j) % n_col)
+        ).start()
     if n_row > 1:
         send_line(n_row - 1)
 
@@ -288,18 +296,22 @@
 
     lax.fori_loop(0, rb // 64, clear, 0)
 
-    landed(stat_a.at[pl.ds(0, n_col - 1)], once.at[6])
+    landed(sums_a.at[pl.ds(0, n_z - 1)], once.at[13])
+    total_a[:, near] = jnp.sum(sums_a[...], 0)
+    swap_a = remote(total_a.at[:, near], total_a.at[:, near], once.at[14], once.at[15], beside)
+    swap_a.start()
     landed(stat_b.at[pl.ds(0, n_row - 1)], once.at[9])
 
-    def coefs(stat, coef):
-        sums = jnp.sum(stat[...], 0)
+    def coefs(sums, coef):
         mean = sums[0:1] / count
         var = sums[1:2] / count - mean * mean
         coef[0:1, :] = mean
         coef[1:2, :] = lax.rsqrt(var + 1e-05)
 
-    coefs(stat_a, coef_a)
-    coefs(stat_b, coef_b)
+    coefs(jnp.sum(stat_b[...], 0), coef_b)
+    swap_a.wait_send()
+    landed(total_a.at[:, away], once.at[15])
+    coefs(total_a[...], coef_a)
 
     tile = min(1024, rb)
 
@@ -381,15 +393,23 @@
                 rows = pl.ds(pl.multiple_of(p * t, t), t)
                 normalize_b(zz, rows, t)
 
-                def some(f, carry):
+                def take(f):
                     landed(slab(g, p, f), r_tail.at[f])
                     tail_across(g, p, f).start()
+
+                def use(f):
                     landed(slab(other, p, f), x_tail.at[f])
                     cols = pl.ds(pl.multiple_of(f * wide, wide), wide)
                     out[cols, :] = finish(out[cols, :] + product(zz, rows, t, cols, wide))
+
+                def some(f, carry):
+                    take(f)
+                    use(f - 1)
                     return carry
 
-                lax.fori_loop(0, TAIL, some, 0)
+                take(0)
+                lax.fori_loop(1, TAIL, some, 0)
+                use(TAIL - 1)
 
     def step(d, carry):
         process_all(d)
@@ -425,70 +445,51 @@
     folded = partial[:, 0:128]
     for q in range(1, cb // 128):
         folded = folded + partial[:, q * 128 : (q + 1) * 128]
-    folded = jnp.sum(0.0051 * folded, 0, keepdims=True)
-
-    def diagonal(q, carry):
-        first = c * cb + q * 128 - r * rb
-        inside = jnp.logical_and(first >= 0, first < rb)
-        rows = pl.ds(pl.multiple_of(jnp.where(inside, first, 0), 128), 128)
-        x = out[rows, pl.ds(pl.multiple_of(q * 128, 128), 128)]
+    shares[me] = jnp.sum(0.0051 * folded, 0, keepdims=True)
+    first = c * cb - r * rb
+
+    @pl.when(jnp.logical_and(first > -cb, first < rb))
+    def _():
         same = lax.broadcasted_iota(jnp.int32, (128, 128), 0) == lax.broadcasted_iota(
             jnp.int32, (128, 128), 1
         )
-        more = jnp.where(
-            jnp.logical_and(same, inside), (1.0 - x) * (1.0 - x) - 0.0051 * (x * x), 0.0
-        )
-        return carry + jnp.sum(more, 0, keepdims=True)
-
-    folded = lax.fori_loop(0, cb // 128, diagonal, folded)
-    n_dev = n_row * n_col
-    me = r * n_col + c
-    shares[me] = folded
-
-    def send_share(i):
-        dst = (me + i) % n_dev
-        ref = shares.at[me]
-        return remote(ref, ref, once.at[10], once.at[11], (dst // n_col, dst % n_col))
-
-    def each_peer(do):
-        def one(i, carry):
-            do(i)
-            return carry
-
-        lax.fori_loop(1, n_dev, one, 0)
-
-    each_peer(lambda i: send_share(i).start())
+
+        def diagonal(q, carry):
+            at = first + q * 128
+            inside = jnp.logical_and(at >= 0, at < rb)
+            rows = pl.ds(pl.multiple_of(jnp.where(inside, at, 0), 128), 128)
+            x = out[rows, pl.ds(pl.multiple_of(q * 128, 128), 128)]
+            more = (1.0 - x) * (1.0 - x) - 0.0051 * (x * x)
+            return carry + jnp.where(jnp.logical_and(same, inside), more, 0.0)
+
+        found = lax.fori_loop(0, cb // 128, diagonal, jnp.zeros((128, 128), F32))
+        shares[me] += jnp.sum(found, 0, keepdims=True)
+
+
+    for i, j in reversed(peers):
+        remote(shares.at[me], shares.at[me], once.at[10], once.at[11], (row_mate(i), col_mate(j))).start()
 
     sent(a_all.at[0, pl.ds(0, (n_row - 1) * t)], once.at[2])
     sent(b_all.at[pl.ds(0, n_col - 1), pl.ds(0, t)], once.at[3])
-    sent(stat_a.at[pl.ds(0, n_col - 1)], once.at[5])
+    sent(sums_a.at[pl.ds(0, n_z - 1)], once.at[12])
     sent(stat_b.at[pl.ds(0, n_row - 1)], once.at[8])
     sent(b_all.at[:, pl.ds(0, (n_row - 1) * t)], once.at[7])
     sent(a_all.at[pl.ds(0, n_z)], once.at[4])
 
-    def drain(zz, carry):
-        whole = a_all.at[0]
-        most = a_all.at[0, pl.ds(0, (n_row - 1) * t)]
-        for way in range(2):
-            sends = jnp.logical_and(zz <= z, can_up) if way == 0 else jnp.logical_and(zz >= z, can_down)
-            cut = jnp.logical_and(n_z > 2, (z - zz if way == 0 else zz - z) == n_z - 2)
-
-            @pl.when(jnp.logical_and(sends, jnp.logical_not(cut)))
-            def _():
-                sent(whole, s_line.at[way, zz])
-
-            @pl.when(jnp.logical_and(sends, cut))
-            def _():
-                sent(most, s_line.at[way, zz])
-                sent(a_all.at[0, pl.ds(0, t)], s_tail.at[way])
-
-        return carry
-
-    lax.fori_loop(0, n_z, drain, 0)
-
+    ends = jnp.logical_or(z == 0, z == n_z - 1)
+
+    @pl.when(ends)
+    def _():
+        sent(a_all.at[0], once.at[16])
+
+    if n_z > 2:
+        @pl.when(jnp.logical_not(ends))
+        def _():
+            sent(a_all.at[pl.ds(0, n_z + 1)], once.at[16])
+
+    sent(shares.at[pl.ds(0, n_dev - 1)], once.at[10])
     landed(shares.at[pl.ds(0, n_dev - 1)], once.at[11])
     loss_out[...] = jnp.sum(jnp.sum(shares[...], 0), keepdims=True) / width
-    sent(shares.at[pl.ds(0, n_dev - 1)], once.at[10])
 
 
 def hbm(x):
@@ -542,16 +543,18 @@
             pltpu.VMEM((n_col, n_chunk, rb), BF16),
             pltpu.VMEM((n_col, n_chunk, cb), BF16),
             pltpu.VMEM((2 * n_chunk, cb), BF16),
-            pltpu.VMEM((n_col, 2, rb), F32),
+            pltpu.VMEM((2, 2, rb), F32),
+            pltpu.VMEM((n_col // 2, 2, rb // 2), F32),
+            pltpu.VMEM((2, rb), F32),
             pltpu.VMEM((n_row, 2, cb), F32),
             pltpu.VMEM((2, rb), F32),
             pltpu.VMEM((2, cb), F32),
             pltpu.VMEM((8, cb), F32),
             pltpu.VMEM((n_row * n_col, 1, 128), F32),
             dma((n_row,)), dma((n_col // 2,)),
-            dma((2, n_col // 2)), dma((n_col // 2, n_row)), dma((n_col // 2 + n_row,)),
-            dma((2,)), dma((TAIL,)), dma((TAIL,)),
-            dma((n_col // 2,)), dma((12,)),
+            dma((n_col // 2, n_row)), dma((n_col // 2 + n_row,)),
+            dma((TAIL,)), dma((TAIL,)),
+            dma((n_col // 2,)), dma((17,)),
         ],
         compiler_params=pltpu.CompilerParams(
             collective_id=0, has_side_effects=True, vmem_limit_bytes=min(size + (12 << 20), 60 << 20)

time: 150 us -> 147 us (0.980)
  Pallas kernels: 147 us -> 145 us
    pallas_call x1, Pallas kernels: 144 us -> 141 us  [shards(): pl.pallas_call(functools.partial(body, n_row, n_col, width), out_shape=(j...]
where the time goes in v3:
time: 147 us
  Pallas kernels  145 us (99%)
  between operations  2.33 us (2%)
    pallas_call x1, Pallas kernels, shards(): pl.pallas_call(functools.partial(body, n_row, n_col, width), out_shape=(j...  141 us
    pallas_call x1, Pallas kernels, emit(): pl.pallas_call(functools.partial(emit_body, 8), out_shape=jax.ShapeDtypeS...  3.37 us

profile of v3, /device:TPU:0, one launch (start us, length us, event | category | flops | bytes accessed | tf_op | source)
XLA Modules:
  0.0 147.1 jit_solution(18031080897005520877)
XLA Ops:
  0.6 141.4 %twins.1 = (f32[2048,1024]{1,0:T(8,128)S(1)}, f32[1,1]{1,0:T(1,128)}) custom-call(bf16[96,8192]{1,0:T(8,128)(2,1)} %a_in.1, bf16[96,8192]{1,0:T(8,128)(2,1)} %b_in.1), custom_call_target="tpu_custom_call" | custom-call | tf_op jit(solution)/shard_map/twins/pallas_call | solution.py:534
  142.0 3.4 %emit.1 = f32[2048,1024]{1,0:T(8,128)} custom-call(f32[2048,1024]{1,0:T(8,128)S(1)} %get-tuple-element.4.x), custom_call_target="tpu_custom_call" | custom-call | tf_op jit(solution)/shard_map/emit/pallas_call | solution.py:513

commit v4 on v3

--- a/solution.py
+++ b/solution.py
@@ -14,8 +14,8 @@
 
 
 def body(
-    n_row, n_col, width,
-    a_in, b_in, out, loss_out,
+    n_row, n_col,
+    a_in, b_in, out, shares_out,
     a_all, b_all, nb, stat_a, sums_a, total_a, stat_b, coef_a, coef_b, partial, shares,
     r_a, r_b, r_line, r_across, r_tail, x_tail, r_fwd, once,
 ):
@@ -82,9 +82,6 @@
         cols = pl.ds(pl.multiple_of(dst * cb, cb), cb)
         return remote(b_in.at[:, cols], b_all.at[c, mine], once.at[3], r_b.at[z], (r, dst))
 
-    for i in range(1, n_row):
-        send_a(i).start()
-
     def block(chunk, p):
         return a_all.at[chunk, pl.ds(pl.multiple_of(p * t, t), t)]
 
@@ -99,7 +96,7 @@
 
     def down(chunk, p):
         ref = block(chunk, p)
-        return remote(ref, ref, once.at[16], r_line.at[chunk // 2, p], below)
+        return remote(ref, ref, once.at[16], r_line.at[chunk // 2 - 1, p], below)
 
     def across(chunk, p):
         ref = block(chunk, p)
@@ -143,6 +140,8 @@
 
     own_a.wait()
     send_line(0)
+    for i in range(1, n_row):
+        send_a(i).start()
 
     for dist in range(n_z - 1, 0, -1):
         for side in range(2):
@@ -381,7 +380,7 @@
 
             def one(o, carry):
                 p = slice_at(o)
-                up(g, p).wait_recv()
+                landed(block(g, p), r_line.at[jnp.where(z == 0, n_z - 2, 0), p])
                 across(g, p).start()
                 landed(block(other, p), r_across.at[n_z + p])
                 multiply(zz, pl.ds(pl.multiple_of(p * t, t), t), t)
@@ -466,8 +465,11 @@
         shares[me] += jnp.sum(found, 0, keepdims=True)
 
 
-    for i, j in reversed(peers):
-        remote(shares.at[me], shares.at[me], once.at[10], once.at[11], (row_mate(i), col_mate(j))).start()
+    way = jnp.where(2 * z >= n_z, 1, n_col - 1)
+    far_first = sorted(peers, key=lambda ij: (ij[1] == 0, (ij[1] - 2) % n_col, ij[0] % 2 == 0))
+    for i, j in far_first:
+        to = (row_mate(i), (c + way * j) % n_col)
+        remote(shares.at[me], shares.at[me], once.at[10], once.at[11], to).start()
 
     sent(a_all.at[0, pl.ds(0, (n_row - 1) * t)], once.at[2])
     sent(b_all.at[pl.ds(0, n_col - 1), pl.ds(0, t)], once.at[3])
@@ -489,36 +491,35 @@
 
     sent(shares.at[pl.ds(0, n_dev - 1)], once.at[10])
     landed(shares.at[pl.ds(0, n_dev - 1)], once.at[11])
-    loss_out[...] = jnp.sum(jnp.sum(shares[...], 0), keepdims=True) / width
+    shares_out[...] = shares[...]
 
 
 def hbm(x):
     return pltpu.with_memory_space_constraint(x, pltpu.HBM)
 
 
-def emit_body(pieces, x, out, sem):
+def emit_body(pieces, width, x, shares, out, loss_out, loss, sem):
     height = x.shape[0] // pieces
-
-    def move(i):
+    for i in range(pieces):
         rows = pl.ds(i * height, height)
-        return pltpu.make_async_copy(x.at[rows], out.at[rows], sem.at[i])
-
-    for i in range(pieces):
-        move(i).start()
-    for i in range(pieces):
-        move(i).wait()
-
-
-def emit(x):
+        pltpu.make_async_copy(x.at[rows], out.at[rows], sem.at[0]).start()
+    loss[...] = jnp.sum(jnp.sum(shares[...], 0), keepdims=True) / width
+    send_loss = pltpu.make_async_copy(loss, loss_out, sem.at[1])
+    send_loss.start()
+    pltpu.make_async_copy(x, out, sem.at[0]).wait()
+    send_loss.wait()
+
+
+def emit(x, shares, width):
     return pl.pallas_call(
-        functools.partial(emit_body, 8),
-        out_shape=jax.ShapeDtypeStruct(x.shape, x.dtype),
-        in_specs=[pl.BlockSpec(memory_space=pltpu.VMEM)],
-        out_specs=pl.BlockSpec(memory_space=pltpu.HBM),
-        scratch_shapes=[pltpu.SemaphoreType.DMA((8,))],
+        functools.partial(emit_body, 8, width),
+        out_shape=(jax.ShapeDtypeStruct(x.shape, x.dtype), jax.ShapeDtypeStruct((1, 1), F32)),
+        in_specs=[pl.BlockSpec(memory_space=pltpu.VMEM)] * 2,
+        out_specs=(pl.BlockSpec(memory_space=pltpu.HBM),) * 2,
+        scratch_shapes=[pltpu.VMEM((1, 1), F32), pltpu.SemaphoreType.DMA((2,))],
         compiler_params=pltpu.CompilerParams(vmem_limit_bytes=16 << 20),
         name="emit",
-    )(x)
+    )(x, shares)
 
 
 def shards(view_a, view_b):
@@ -531,11 +532,11 @@
     n_chunk = t * n_row
     dma = pltpu.SemaphoreType.DMA
     size = 2 * (count * (rb + cb) + 2 * n_chunk * cb + 2 * t * width) + 4 * rb * cb
-    product, loss = pl.pallas_call(
-        functools.partial(body, n_row, n_col, width),
+    product, shares = pl.pallas_call(
+        functools.partial(body, n_row, n_col),
         out_shape=(
             jax.ShapeDtypeStruct((rb, cb), F32),
-            jax.ShapeDtypeStruct((1, 1), F32),
+            jax.ShapeDtypeStruct((n_row * n_col, 1, 128), F32),
         ),
         in_specs=[pl.BlockSpec(memory_space=pltpu.HBM)] * 2,
         out_specs=(pl.BlockSpec(memory_space=pltpu.VMEM),) * 2,
@@ -552,7 +553,7 @@
             pltpu.VMEM((8, cb), F32),
             pltpu.VMEM((n_row * n_col, 1, 128), F32),
             dma((n_row,)), dma((n_col // 2,)),
-            dma((n_col // 2, n_row)), dma((n_col // 2 + n_row,)),
+            dma((max(n_col // 2 - 1, 1), n_row)), dma((n_col // 2 + n_row,)),
             dma((TAIL,)), dma((TAIL,)),
             dma((n_col // 2,)), dma((17,)),
         ],
@@ -561,7 +562,8 @@
         ),
         name="twins",
     )(hbm(view_a), hbm(view_b))
-    return emit(product), loss.reshape(())
+    product, loss = emit(product, shares, width)
+    return product, loss.reshape(())
 
 
 def solution(mesh):

time: 147 us -> 145 us (0.986)
  between operations: 2.33 us -> 0.64 us
where the time goes in v4:
time: 145 us
  Pallas kernels  144 us (99%)
    pallas_call x1, Pallas kernels, shards(): pl.pallas_call(functools.partial(body, n_row, n_col), out_shape=(jax.Shap...  141 us
    pallas_call x1, Pallas kernels, emit(): pl.pallas_call(functools.partial(emit_body, 8, width), out_shape=(jax.Sha...  3.32 us

profile of v4, /device:TPU:0, one launch (start us, length us, event | category | flops | bytes accessed | tf_op | source)
XLA Modules:
  0.0 144.7 jit_solution(13014138491367400384)
XLA Ops:
  0.6 140.7 %twins.1 = (f32[2048,1024]{1,0:T(8,128)S(1)}, f32[32,1,128]{2,1,0:T(1,128)S(1)}) custom-call(bf16[96,8192]{1,0:T(8,128)(2,1)} %a_in.1, bf16[96,8192]{1,0:T(8,128)(2,1)} %b_in.1), custom_call_target="tpu_custom_call" | custom-call | tf_op jit(solution)/shard_map/twins/pallas_call | solution.py:535
  141.4 3.3 %emit.1 = (f32[2048,1024]{1,0:T(8,128)}, f32[1,1]{1,0:T(1,128)}) custom-call(f32[2048,1024]{1,0:T(8,128)S(1)} %get-tuple-element.6.x, f32[32,1,128]{2,1,0:T(1,128)S(1)} %get-tuple-element.7.shares), custom_call_target="tpu_custom_call" | custom-call | tf_op jit(solution)/shard_map/emit/pallas_call | solution.py:514

commit v5 on v4

--- a/solution.py
+++ b/solution.py
@@ -16,7 +16,7 @@
 def body(
     n_row, n_col,
     a_in, b_in, out, shares_out,
-    a_all, b_all, nb, stat_a, sums_a, total_a, stat_b, coef_a, coef_b, partial, shares,
+    a_all, b_all, nb, stat_a, sums_a, total_a, stat_b, coef_a, coef_b, partial, spread, shares,
     r_a, r_b, r_line, r_across, r_tail, x_tail, r_fwd, once,
 ):
     t = a_in.shape[0]
@@ -104,12 +104,11 @@
         slot = jnp.where(far, n_z + p, chunk // 2)
         return remote(ref, ref, once.at[4], r_across.at[slot], beside)
 
-    wide = rb // TAIL
+    widths = [rb >> min(f + 1, TAIL - 1) for f in range(TAIL)]
+    slabs = [pl.ds(sum(widths[:f]), widths[f]) for f in range(TAIL)]
 
     def slab(chunk, p, f):
-        return a_all.at[
-            chunk, pl.ds(pl.multiple_of(p * t, t), t), pl.ds(pl.multiple_of(f * wide, wide), wide)
-        ]
+        return a_all.at[chunk, pl.ds(pl.multiple_of(p * t, t), t), slabs[f]]
 
     def tail(way, chunk, p, f):
         ref = slab(chunk, p, f)
@@ -369,6 +368,27 @@
         partial[...] += jnp.sum((x * x).reshape(x.shape[0] // 8, 8, cb), 0)
         return x
 
+    first = c * cb - r * rb
+
+    def diagonal(start, height):
+        @pl.when(jnp.logical_and(first > start - cb, first < start + height))
+        def _():
+            same = lax.broadcasted_iota(jnp.int32, (128, 128), 0) == lax.broadcasted_iota(
+                jnp.int32, (128, 128), 1
+            )
+
+            def one(q, carry):
+                row = start + q * 128
+                col = row - first
+                inside = jnp.logical_and(col >= 0, col < cb)
+                cols = pl.ds(pl.multiple_of(jnp.where(inside, col, 0), 128), 128)
+                x = out[pl.ds(pl.multiple_of(row, 128), 128), cols]
+                more = (1.0 - x) * (1.0 - x) - 0.0051 * (x * x)
+                more = jnp.where(jnp.logical_and(same, inside), more, 0.0)
+                return carry + jnp.sum(more.reshape(16, 8, 128), 0)
+
+            spread[...] += lax.fori_loop(0, height // 128, one, jnp.zeros((8, 128), F32))
+
     def last():
         zz = jnp.where(z == 0, n_z - 1, 0)
         g = zz * 2 + k
@@ -398,16 +418,14 @@
 
                 def use(f):
                     landed(slab(other, p, f), x_tail.at[f])
-                    cols = pl.ds(pl.multiple_of(f * wide, wide), wide)
-                    out[cols, :] = finish(out[cols, :] + product(zz, rows, t, cols, wide))
-
-                def some(f, carry):
+                    cols = slabs[f]
+                    out[cols, :] = finish(out[cols, :] + product(zz, rows, t, cols, widths[f]))
+                    diagonal(slabs[f].start, widths[f])
+
+                take(0)
+                for f in range(1, TAIL):
                     take(f)
                     use(f - 1)
-                    return carry
-
-                take(0)
-                lax.fori_loop(1, TAIL, some, 0)
                 use(TAIL - 1)
 
     def step(d, carry):
@@ -429,6 +447,7 @@
 
     lax.fori_loop(0, max(n_z - 1, 1), step, 0)
     partial[...] = jnp.zeros((8, cb), F32)
+    spread[...] = jnp.zeros((8, 128), F32)
     if n_z > 1:
         last()
 
@@ -440,30 +459,12 @@
             return carry
 
         lax.fori_loop(0, rb // 64, part, 0)
+        diagonal(0, rb)
 
     folded = partial[:, 0:128]
     for q in range(1, cb // 128):
         folded = folded + partial[:, q * 128 : (q + 1) * 128]
-    shares[me] = jnp.sum(0.0051 * folded, 0, keepdims=True)
-    first = c * cb - r * rb
-
-    @pl.when(jnp.logical_and(first > -cb, first < rb))
-    def _():
-        same = lax.broadcasted_iota(jnp.int32, (128, 128), 0) == lax.broadcasted_iota(
-            jnp.int32, (128, 128), 1
-        )
-
-        def diagonal(q, carry):
-            at = first + q * 128
-            inside = jnp.logical_and(at >= 0, at < rb)
-            rows = pl.ds(pl.multiple_of(jnp.where(inside, at, 0), 128), 128)
-            x = out[rows, pl.ds(pl.multiple_of(q * 128, 128), 128)]
-            more = (1.0 - x) * (1.0 - x) - 0.0051 * (x * x)
-            return carry + jnp.where(jnp.logical_and(same, inside), more, 0.0)
-
-        found = lax.fori_loop(0, cb // 128, diagonal, jnp.zeros((128, 128), F32))
-        shares[me] += jnp.sum(found, 0, keepdims=True)
-
+    shares[me] = jnp.sum(0.0051 * folded + spread[...], 0, keepdims=True)
 
     way = jnp.where(2 * z >= n_z, 1, n_col - 1)
     far_first = sorted(peers, key=lambda ij: (ij[1] == 0, (ij[1] - 2) % n_col, ij[0] % 2 == 0))
@@ -551,6 +552,7 @@
             pltpu.VMEM((2, rb), F32),
             pltpu.VMEM((2, cb), F32),
             pltpu.VMEM((8, cb), F32),
+            pltpu.VMEM((8, 128), F32),
             pltpu.VMEM((n_row * n_col, 1, 128), F32),
             dma((n_row,)), dma((n_col // 2,)),
             dma((max(n_col // 2 - 1, 1), n_row)), dma((n_col // 2 + n_row,)),

time: 145 us -> 145 us (level)
  no operation moved by 1% of the time
where the time goes in v5:
time: 145 us
  Pallas kernels  144 us (99%)
    pallas_call x1, Pallas kernels, shards(): pl.pallas_call(functools.partial(body, n_row, n_col), out_shape=(jax.Shap...  141 us
    pallas_call x1, Pallas kernels, emit(): pl.pallas_call(functools.partial(emit_body, 8, width), out_shape=(jax.Sha...  3.32 us

profile of v5, /device:TPU:0, one launch (start us, length us, event | category | flops | bytes accessed | tf_op | source)
XLA Modules:
  0.0 144.5 jit_solution(5148804007619768400)
XLA Ops:
  0.6 140.6 %twins.1 = (f32[2048,1024]{1,0:T(8,128)S(1)}, f32[32,1,128]{2,1,0:T(1,128)S(1)}) custom-call(bf16[96,8192]{1,0:T(8,128)(2,1)} %a_in.1, bf16[96,8192]{1,0:T(8,128)(2,1)} %b_in.1), custom_call_target="tpu_custom_call" | custom-call | tf_op jit(solution)/shard_map/twins/pallas_call | solution.py:536
  141.2 3.3 %emit.1 = (f32[2048,1024]{1,0:T(8,128)}, f32[1,1]{1,0:T(1,128)}) custom-call(f32[2048,1024]{1,0:T(8,128)S(1)} %get-tuple-element.6.x, f32[32,1,128]{2,1,0:T(1,128)S(1)} %get-tuple-element.7.shares), custom_call_target="tpu_custom_call" | custom-call | tf_op jit(solution)/shard_map/emit/pallas_call | solution.py:515

commit v6 on v5

--- a/solution.py
+++ b/solution.py
@@ -423,10 +423,12 @@
                     diagonal(slabs[f].start, widths[f])
 
                 take(0)
+                take(1)
+                use(0)
+                for f in range(2, TAIL):
+                    take(f)
                 for f in range(1, TAIL):
-                    take(f)
-                    use(f - 1)
-                use(TAIL - 1)
+                    use(f)
 
     def step(d, carry):
         process_all(d)

time: 145 us -> 144 us (level)
  no operation moved by 1% of the time
where the time goes in v6:
time: 144 us
  Pallas kernels  144 us (100%)
    pallas_call x1, Pallas kernels, shards(): pl.pallas_call(functools.partial(body, n_row, n_col), out_shape=(jax.Shap...  140 us
    pallas_call x1, Pallas kernels, emit(): pl.pallas_call(functools.partial(emit_body, 8, width), out_shape=(jax.Sha...  3.32 us

profile of v6, /device:TPU:0, one launch (start us, length us, event | category | flops | bytes accessed | tf_op | source)
XLA Modules:
  0.0 144.3 jit_solution(15564777353148403644)
XLA Ops:
  0.6 140.4 %twins.1 = (f32[2048,1024]{1,0:T(8,128)S(1)}, f32[32,1,128]{2,1,0:T(1,128)S(1)}) custom-call(bf16[96,8192]{1,0:T(8,128)(2,1)} %a_in.1, bf16[96,8192]{1,0:T(8,128)(2,1)} %b_in.1), custom_call_target="tpu_custom_call" | custom-call | tf_op jit(solution)/shard_map/twins/pallas_call | solution.py:538
  141.0 3.3 %emit.1 = (f32[2048,1024]{1,0:T(8,128)}, f32[1,1]{1,0:T(1,128)}) custom-call(f32[2048,1024]{1,0:T(8,128)S(1)} %get-tuple-element.6.x, f32[32,1,128]{2,1,0:T(1,128)S(1)} %get-tuple-element.7.shares), custom_call_target="tpu_custom_call" | custom-call | tf_op jit(solution)/shard_map/emit/pallas_call | solution.py:517

commit v7 on v5

--- a/solution.py
+++ b/solution.py
@@ -10,7 +10,10 @@
 MESH = pl.DeviceIdType.MESH
 F32 = jnp.float32
 BF16 = jnp.bfloat16
-TAIL = 4
+
+
+def tail_slabs(rb):
+    return min(5, (rb // 128).bit_length())
 
 
 def body(
@@ -104,8 +107,9 @@
         slot = jnp.where(far, n_z + p, chunk // 2)
         return remote(ref, ref, once.at[4], r_across.at[slot], beside)
 
-    widths = [rb >> min(f + 1, TAIL - 1) for f in range(TAIL)]
-    slabs = [pl.ds(sum(widths[:f]), widths[f]) for f in range(TAIL)]
+    n_tail = tail_slabs(rb)
+    widths = [rb >> min(f + 1, n_tail - 1) for f in range(n_tail)]
+    slabs = [pl.ds(sum(widths[:f]), widths[f]) for f in range(n_tail)]
 
     def slab(chunk, p, f):
         return a_all.at[chunk, pl.ds(pl.multiple_of(p * t, t), t), slabs[f]]
@@ -218,7 +222,7 @@
             @pl.when(can_up)
             def _():
                 if split:
-                    for f in range(TAIL):
+                    for f in range(n_tail):
                         tail(0, low, p, f).start()
                 else:
                     up(low, p).start()
@@ -232,7 +236,7 @@
             @pl.when(can_down)
             def _():
                 if split:
-                    for f in range(TAIL):
+                    for f in range(n_tail):
                         tail(1, high, p, f).start()
                 else:
                     down(high, p).start()
@@ -423,10 +427,10 @@
                     diagonal(slabs[f].start, widths[f])
 
                 take(0)
-                for f in range(1, TAIL):
+                for f in range(1, n_tail):
                     take(f)
                     use(f - 1)
-                use(TAIL - 1)
+                use(n_tail - 1)
 
     def step(d, carry):
         process_all(d)
@@ -556,7 +560,7 @@
             pltpu.VMEM((n_row * n_col, 1, 128), F32),
             dma((n_row,)), dma((n_col // 2,)),
             dma((max(n_col // 2 - 1, 1), n_row)), dma((n_col // 2 + n_row,)),
-            dma((TAIL,)), dma((TAIL,)),
+            dma((tail_slabs(rb),)), dma((tail_slabs(rb),)),
             dma((n_col // 2,)), dma((17,)),
         ],
         compiler_params=pltpu.CompilerParams(

time: 145 us -> 145 us (level)
  no operation moved by 1% of the time
where the time goes in v7:
time: 145 us
  Pallas kernels  145 us (100%)
    pallas_call x1, Pallas kernels, shards(): pl.pallas_call(functools.partial(body, n_row, n_col), out_shape=(jax.Shap...  141 us
    pallas_call x1, Pallas kernels, emit(): pl.pallas_call(functools.partial(emit_body, 8, width), out_shape=(jax.Sha...  3.32 us

profile of v7, /device:TPU:0, one launch (start us, length us, event | category | flops | bytes accessed | tf_op | source)
XLA Modules:
  0.0 145.2 jit_solution(604226830535806771)
XLA Ops:
  0.6 141.3 %twins.1 = (f32[2048,1024]{1,0:T(8,128)S(1)}, f32[32,1,128]{2,1,0:T(1,128)S(1)}) custom-call(bf16[96,8192]{1,0:T(8,128)(2,1)} %a_in.1, bf16[96,8192]{1,0:T(8,128)(2,1)} %b_in.1), custom_call_target="tpu_custom_call" | custom-call | tf_op jit(solution)/shard_map/twins/pallas_call | solution.py:540
  141.9 3.3 %emit.1 = (f32[2048,1024]{1,0:T(8,128)}, f32[1,1]{1,0:T(1,128)}) custom-call(f32[2048,1024]{1,0:T(8,128)S(1)} %get-tuple-element.6.x, f32[32,1,128]{2,1,0:T(1,128)S(1)} %get-tuple-element.7.shares), custom_call_target="tpu_custom_call" | custom-call | tf_op jit(solution)/shard_map/emit/pallas_call | solution.py:519
